TPU v7x, 128 devices: a whole 4x4x4 slice. The times are simulated.
128 devices in a mesh: dp: 16 (over z, y), ep: 8 (over x, core).
Axes of the slice: x: 4, y: 4, z: 4, core: 2. Of those that a mesh axis runs over, the one named last changes fastest.
Arguments:
- x: bfloat16 [98304, 768], P(('dp', 'ep'))
- gy: bfloat16 [98304, 768], P(('dp', 'ep'))
- idx: int32 [98304], P(('dp', 'ep'))
- w_gate: bfloat16 [768, 16], replicated
- w_up: bfloat16 [16, 768, 3072], P('ep')
- w_down: bfloat16 [16, 3072, 768], P('ep')
Outputs:
- output 1: bfloat16 [98304, 768], P(('dp', 'ep'))
- output 2: bfloat16 [98304, 768], P(('dp', 'ep'))
- output 3: float32 [16, 768, 3072], P('ep')
- output 4: float32 [16, 3072, 768], P('ep')
- output 5: float32 [768, 16], replicated
All inputs are finite; a program needn't handle non-finite values.
Results may differ from a plain program's by a relative error of at most 0.00584019.
Values are sent between devices in bfloat16 or wider.
A program may use at most 1 GiB of HBM per device.

v0:
```python
import jax
import jax.numpy as jnp
from jax import lax
from jax.sharding import PartitionSpec as P

PAD_FACTOR = 4


def solution(mesh):
    ep_size = mesh.shape['ep']
    tok_spec = P(('dp', 'ep'), None)
    idx_spec = P(('dp', 'ep'))
    rep_spec = P(None, None)
    exp_spec = P('ep', None, None)

    def local_step(x_loc, gy_loc, idx_loc, w_gate, w_up, w_down):
        tok_count, d_model = x_loc.shape
        n_experts = w_gate.shape[1]
        local_experts = w_up.shape[0]
        cap_rows = PAD_FACTOR * tok_count // n_experts
        onehot = idx_loc[:, None] == jnp.arange(n_experts, dtype=jnp.int32)[None, :]
        expert_count = jnp.sum(onehot, axis=0, dtype=jnp.int32)
        sort_order = jnp.argsort(idx_loc, stable=True)
        sorted_pos = jnp.argsort(sort_order)
        expert_start = jnp.cumsum(expert_count) - expert_count
        slot_k = jnp.arange(cap_rows, dtype=jnp.int32)
        slot_valid = slot_k[None, :] < expert_count[:, None]
        src_tok = sort_order[jnp.minimum(expert_start[:, None] + slot_k[None, :], tok_count - 1)]
        slot_tok = idx_loc * cap_rows + sorted_pos - expert_start[idx_loc]

        def dispatch(tok_rows):
            picked = jnp.where(slot_valid[:, :, None], tok_rows[src_tok], jnp.zeros((), tok_rows.dtype))
            picked = picked.reshape(ep_size, local_experts, cap_rows, d_model)
            return lax.all_to_all(picked, 'ep', 0, 0, tiled=True)

        def combine(expert_rows):
            returned = lax.all_to_all(expert_rows, 'ep', 1, 0, tiled=True)
            return returned.reshape(n_experts * cap_rows, d_model)[slot_tok]

        router_logit = jnp.dot(x_loc, w_gate, preferred_element_type=jnp.float32)
        router_prob = jax.nn.softmax(router_logit, axis=-1)
        gate_val = n_experts * jnp.sum(jnp.where(onehot, router_prob, 0.0), axis=1)
        recv_rows = dispatch(x_loc)
        pre_act = jnp.einsum('sekd,edf->eskf', recv_rows, w_up, preferred_element_type=jnp.float32)
        hid_full, gelu_back = jax.vjp(jax.nn.gelu, pre_act)
        hidden = hid_full.astype(jnp.bfloat16)
        expert_out = jnp.einsum('eskf,efd->eskd', hidden, w_down, preferred_element_type=jnp.float32).astype(jnp.bfloat16)
        y_tok = combine(expert_out)
        gy_full = gy_loc.astype(jnp.float32)
        moe_out = (gate_val[:, None] * y_tok.astype(jnp.float32)).astype(jnp.bfloat16)

        dy_tok = (gate_val[:, None] * gy_full).astype(jnp.bfloat16)
        recv_grad = dispatch(dy_tok)
        d_hidden = jnp.einsum('sekd,efd->eskf', recv_grad, w_down, preferred_element_type=jnp.float32)
        d_pre = gelu_back(d_hidden)[0].astype(jnp.bfloat16)
        grad_down = jnp.einsum('eskf,sekd->efd', hidden, recv_grad, preferred_element_type=jnp.float32)
        grad_up = jnp.einsum('sekd,eskf->edf', recv_rows, d_pre, preferred_element_type=jnp.float32)
        d_rows = jnp.einsum('eskf,edf->eskd', d_pre, w_up, preferred_element_type=jnp.float32).astype(jnp.bfloat16)
        dx_expert = combine(d_rows)
        d_gate = jnp.sum(gy_full * y_tok.astype(jnp.float32), axis=1)
        d_logit = ((d_gate * gate_val)[:, None] * (onehot.astype(jnp.float32) - router_prob)).astype(jnp.bfloat16)
        dx_router = jnp.einsum('te,de->td', d_logit, w_gate, preferred_element_type=jnp.float32)
        grad_x = (dx_expert.astype(jnp.float32) + dx_router).astype(jnp.bfloat16)
        grad_gate = jnp.einsum('td,te->de', x_loc, d_logit, preferred_element_type=jnp.float32)
        grad_up = lax.psum(grad_up, 'dp')
        grad_down = lax.psum(grad_down, 'dp')
        grad_gate = lax.psum(grad_gate, ('dp', 'ep'))
        return moe_out, grad_x, grad_up, grad_down, grad_gate

    sharded_fn = jax.shard_map(local_step, mesh=mesh, in_specs=(tok_spec, tok_spec, idx_spec, rep_spec, exp_spec, exp_spec), out_specs=(tok_spec, tok_spec, exp_spec, exp_spec, rep_spec), check_vma=False)
    return sharded_fn
```

profile of v0, /device:TPU:1, one launch (start us, length us, event | category | flops | bytes accessed | tf_op | source)
XLA Modules:
  0.0 869.0 jit_solution(13061245459646268617)
XLA Ops:
  7.2 0.0 copy-start
  7.2 0.9 convert_reduce_fusion
  8.1 0.1 lt.50
  8.2 0.1 iota_compare_fusion.1
  8.3 0.0 copy-start.11
  8.3 5.1 sort.34
  13.3 0.1 copy.19
  13.5 0.1 reduce
  13.6 0.1 compare_select_fusion.1
  13.7 0.1 reshape.142
  13.7 12.6 %gather_fusion = s32[3072]{0:T(1024)S(1)} fusion(s32[768]{0:T(1024)S(1)} %get-tuple-element.7, s32[3072]{0:T(1024)S(1)} %broadcast_clamp_fusion), kind=kCustom, calls=%fused_computation | custom fusion | bytes 36864 | tf_op jit(solution)/shard_map/gather | solution.py:28
  26.4 0.1 gather.25
  26.5 0.1 reshape.150
  26.5 0.0 copy-done
  26.6 13.6 %gather_fusion.1 = bf16[3072,768]{1,0:T(8,128)(2,1)} fusion(bf16[768,768]{1,0:T(8,128)(2,1)S(1)} %copy-done, s32[3072]{0:T(1024)S(1)} %broadcast_clamp_fusion.1), kind=kCustom, calls=%fused_computation.1 | custom fusion | bytes 9449472 | tf_op jit(solution)/shard_map/gather | solution.py:32
  40.1 0.0 copy-done.11
  40.1 2.7 broadcast_select_fusion.1
  42.8 59.9 %all_to_all.40 = bf16[8,2,192,768]{3,2,1,0:T(8,128)(2,1)S(1)} all-to-all(bf16[8,2,192,768]{3,2,1,0:T(8,128)(2,1)S(1)} %broadcast_select_fusion.1), channel_id=1, replica_groups=mesh['dp'=16,'ep'=8] {'ep'}, dimensions={0} | all-to-all | bytes 9437184 | tf_op jit(solution)/shard_map/all_to_all | solution.py:34
  102.7 2.1 copy-done.2
  104.8 23.1 %fusion.11 = f32[2,8,192,3072]{3,2,1,0:T(8,128)} fusion(bf16[2,768,3072]{2,1,0:T(8,128)(2,1)} %param.10, bf16[8,2,192,768]{3,2,1,0:T(8,128)(2,1)S(1)} %all_to_all.40), kind=kOutput, calls=%fused_computation.19 | convolution fusion | flops 14495514624 | bytes 51904512 | tf_op jit(solution)/shard_map/sekd,edf->eskf/dot_general | solution.py:44
  127.9 26.1 %fusion.25 = bf16[2,8,192,768]{3,2,1,0:T(8,128)(2,1)} fusion(bf16[2,3072,768]{2,1,0:T(8,128)(2,1)} %param.11, f32[2,8,192,3072]{3,2,1,0:T(8,128)} %fusion.11), kind=kOutput, calls=%fused_computation.35 | convolution fusion | flops 14582808576 | bytes 51904512 | tf_op jit(solution)/shard_map/eskf,efd->eskd/dot_general | solution.py:47
  153.9 5.0 copy.21
  158.9 5.6 all-to-all-start.1
  164.5 0.2 all-reduce.3.cloned.1.call-start
  164.7 4.4 sort.35
  169.1 0.7 fusion.39
  169.8 0.0 copy-done.5
  169.8 10.1 %compare_select_fusion.2 = s32[768]{0:T(1024)S(1)} fusion(s32[768]{0:T(1024)S(1)} %get-tuple-element.8, s32[768]{0:T(1024)S(1)} %copy-done.5, s32[]{:T(128)} %bitcast.9, s32[]{:T(128)} %bitcast.10, s32[]{:T(128)} %bitcast.11, s32[]{:T(128)} %bitcast.12, s32[]{:T(128)} %bitcast.13, s32[]{:T(128)} %bitcast.14, s32[]{:T(128)} %bitcast.15, s32[]{:T(128)} %bitcast.16, ...), kind=kLoop, calls=%fused_computation.52 | loop fusion | flops 29952 | bytes 9280 | tf_op jit(solution)/shard_map/select_n | solution.py:38
  179.9 0.0 copy-done.9
  179.9 0.0 copy-start.15
  180.0 0.5 fusion.40
  180.4 0.0 copy-start.3
  180.5 0.6 copy-done.3
  181.1 0.6 copy-done.13
  181.6 37.1 %all-to-all-done.1 = bf16[2,8,192,768]{3,2,0,1:T(8,128)(2,1)} async-done(((bf16[2,8,192,768]{3,2,0,1:T(8,128)(2,1)}), bf16[2,8,192,768]{3,2,0,1:T(8,128)(2,1)}, u32[]{:S(2)}, u32[]{:S(2)}) %all-to-all-start.1) | async-done | bytes 4718624 | tf_op jit(solution)/shard_map/all_to_all | solution.py:37
  218.7 0.0 copy-done.7
  218.8 6.3 gather_fusion.2
  225.0 3.5 fusion.33
  228.5 13.6 %gather_fusion.3 = bf16[3072,768]{1,0:T(8,128)(2,1)} fusion(bf16[768,768]{1,0:T(8,128)(2,1)S(1)} %get-tuple-element.12, s32[3072]{0:T(1024)S(1)} %broadcast_clamp_fusion.1), kind=kCustom, calls=%fused_computation.3 | custom fusion | bytes 9449472 | tf_op jit(solution)/shard_map/gather | solution.py:32
  242.1 2.7 broadcast_select_fusion
  244.7 58.5 %all_to_all.41 = bf16[8,2,192,768]{3,2,1,0:T(8,128)(2,1)} all-to-all(bf16[8,2,192,768]{3,2,1,0:T(8,128)(2,1)S(1)} %broadcast_select_fusion), channel_id=1, replica_groups=mesh['dp'=16,'ep'=8] {'ep'}, dimensions={0} | all-to-all | bytes 9437184 | tf_op jit(solution)/shard_map/all_to_all | solution.py:34
  303.3 43.6 %fusion.6 = bf16[2,8,192,3072]{3,2,1,0:T(8,128)(2,1)} fusion(f32[2,8,192,3072]{3,2,1,0:T(8,128)} %fusion.11, bf16[2,3072,768]{2,1,0:T(8,128)(2,1)} %param.11, bf16[8,2,192,768]{3,2,1,0:T(8,128)(2,1)} %all_to_all.41), kind=kOutput, calls=%fused_computation.13 | convolution fusion | flops 14684258304 | bytes 70778880 | tf_op jit(solution)/shard_map/sekd,efd->eskf/dot_general | solution.py:54
  346.9 32.9 %convolution_bitcast_fusion = f32[2,3072,768]{2,1,0:T(8,128)} fusion(bf16[8,2,192,768]{3,2,1,0:T(8,128)(2,1)} %all_to_all.41, f32[2,8,192,3072]{3,2,1,0:T(8,128)} %fusion.11), kind=kOutput, calls=%fused_computation.25 | convolution fusion | flops 14580449280 | bytes 61341696 | tf_op jit(solution)/shard_map/eskf,sekd->efd/dot_general | solution.py:56
  379.8 22.5 %fusion.19 = f32[2,768,3072]{2,1,0:T(8,128)} fusion(bf16[8,2,192,768]{3,2,1,0:T(8,128)(2,1)} %copy-done.2, bf16[2,8,192,3072]{3,2,1,0:T(8,128)(2,1)} %fusion.6), kind=kOutput, calls=%fused_computation.26 | convolution fusion | flops 14495514624 | bytes 42467328 | tf_op jit(solution)/shard_map/sekd,eskf->edf/dot_general | solution.py:57
  402.3 0.0 all-reduce.3.cloned.1.call-update
  402.3 20.8 %fusion.28 = bf16[2,8,192,768]{3,2,1,0:T(8,128)(2,1)S(1)} fusion(bf16[2,8,192,3072]{3,2,1,0:T(8,128)(2,1)} %fusion.6, bf16[2,768,3072]{2,1,0:T(8,128)(2,1)} %param.10), kind=kOutput, calls=%fused_computation.36 | convolution fusion | flops 14497873920 | bytes 33030144 | tf_op jit(solution)/shard_map/eskf,edf->eskd/dot_general | solution.py:58
  423.1 0.0 copy-start.4
  423.1 0.0 copy-start.6
  423.1 2.5 copy.23
  425.7 5.8 all-to-all-start.3
  431.5 0.0 copy-done.18
  431.5 0.0 copy-done.4
  431.5 0.0 copy-done.6
  431.5 0.0 copy-done.8
  431.5 0.0 copy-done.14
  431.5 0.3 convolution_bitcast_fusion.1
  431.8 113.0 %psum.23 = f32[768,16]{0,1:T(8,128)} all-reduce(f32[768,16]{0,1:T(8,128)S(1)} %convolution_bitcast_fusion.1), channel_id=1, replica_groups=mesh['dp'=16,'ep'=8] {'dp','ep'}, use_global_device_ids=true, to_apply=%region_10.11 | all-reduce | flops 12288 | bytes 98304 | tf_op jit(solution)/shard_map/psum | solution.py:67
  544.8 0.0 all-to-all-done.3
  544.8 6.3 gather_fusion.4
  551.1 1.5 add_convert_fusion
  552.6 284.2 %all-reduce.3.cloned.1.call-done = (f32[2,768,3072]{2,1,0:T(8,128)}, f32[2,3072,768]{2,1,0:T(8,128)}) async-done(((f32[2,768,3072]{2,1,0:T(8,128)}, f32[2,3072,768]{2,1,0:T(8,128)}), (f32[2,768,3072]{2,1,0:T(8,128)}, f32[2,3072,768]{2,1,0:T(8,128)})) %all-reduce.3.cloned.1.call-update) | async-done | bytes 37748752 | tf_op jit(solution)/shard_map/psum | solution.py:65
  836.8 14.0 %copy.43 = f32[2,768,3072]{2,1,0:T(8,128)} copy(f32[2,768,3072]{2,1,0:T(8,128)} %get-tuple-element.34) | data formatting | bytes 37748736
  850.7 4.4 copy-done.1
  855.1 6.8 copy.44
  (32 shorter events, 0.2 us)
Async XLA Ops:
  7.2 19.4 %copy-start = (bf16[768,768]{1,0:T(8,128)(2,1)S(1)}, bf16[768,768]{1,0:T(8,128)(2,1)}, u32[]{:S(2)}) copy-start(bf16[768,768]{1,0:T(8,128)(2,1)} %param.6) | copy-start | bytes 3538948
  8.3 31.9 %copy-start.11 = (pred[8,2,192]{2,1,0:T(4,128)(4,1)}, pred[8,2,192]{2,1,0:T(4,128)(4,1)S(1)}, u32[]{:S(2)}) copy-start(pred[8,2,192]{2,1,0:T(4,128)(4,1)S(1)} %iota_compare_fusion.1) | copy-start | bytes 9220
  102.7 2.1 copy-start.2
  153.9 15.9 %copy-start.5 = (s32[768]{0:T(1024)S(1)}, s32[768]{0:T(1024)}, u32[]{:S(2)}) copy-start(s32[768]{0:T(1024)} %param.8) | copy-start | bytes 9220
  153.9 26.0 %copy-start.9 = (bf16[768,16]{0,1:T(8,128)(2,1)S(1)}, bf16[768,16]{0,1:T(8,128)(2,1)}, u32[]{:S(2)}) copy-start(bf16[768,16]{0,1:T(8,128)(2,1)} %param.9) | copy-start | bytes 73732
  158.9 59.8 %all-to-all-start.1 = ((bf16[2,8,192,768]{3,2,0,1:T(8,128)(2,1)}), bf16[2,8,192,768]{3,2,0,1:T(8,128)(2,1)}, u32[]{:S(2)}, u32[]{:S(2)}) async-start(bf16[2,8,192,768]{3,2,0,1:T(8,128)(2,1)} %copy.21), calls=%async_computation.1 | async-start | bytes 9437184 | tf_op jit(solution)/shard_map/all_to_all | solution.py:37
  164.5 672.2 %all-reduce.3.cloned.1.call-start = ((), (), s32[]{:S(2)}) async-start(), calls=%async_computation.4 | async-start | bytes 75497472 | tf_op jit(solution)/shard_map/psum | solution.py:65
  179.9 38.8 %copy-start.15 = (s32[1024]{0:T(1024)}, s32[1024]{0:T(1024)S(1)}, u32[]{:S(2)}) copy-start(s32[1024]{0:T(1024)S(1)} %pad_clamp_fusion) | copy-start | bytes 12292
  180.4 0.6 copy-start.3
  180.4 38.3 %copy-start.7 = (f32[768]{0:T(1024)}, f32[768]{0:T(1024)S(1)}, u32[]{:S(2)}) copy-start(f32[768]{0:T(1024)S(1)} %get-tuple-element.30) | copy-start | bytes 9220
  181.1 0.6 copy-start.13
  181.6 37.1 %copy-start.17 = (f32[768]{0:T(1024)}, f32[768]{0:T(1024)S(1)}, u32[]{:S(2)}) copy-start(f32[768]{0:T(1024)S(1)} %select_reduce_fusion) | copy-start | bytes 9220
  228.5 13.6 %copy-start.12 = (pred[8,2,192]{2,1,0:T(4,128)(4,1)S(1)}, pred[8,2,192]{2,1,0:T(4,128)(4,1)}, u32[]{:S(2)}) copy-start(pred[8,2,192]{2,1,0:T(4,128)(4,1)} %copy-done.11) | copy-start | bytes 9220
  423.1 8.4 copy-start.18
  423.1 8.4 copy-start.19
  423.1 8.4 copy-start.4
  423.1 8.4 copy-start.6
  423.1 8.4 copy-start.8
  423.1 8.4 copy-start.14
  423.1 121.7 %copy-start.16 = (s32[1024]{0:T(1024)S(1)}, s32[1024]{0:T(1024)}, u32[]{:S(2)}) copy-start(s32[1024]{0:T(1024)} %copy-done.15) | copy-start | bytes 12292
  425.7 125.4 %copy-start.10 = (bf16[768,16]{0,1:T(8,128)(2,1)S(1)}, bf16[768,16]{0,1:T(8,128)(2,1)}, u32[]{:S(2)}) copy-start(bf16[768,16]{0,1:T(8,128)(2,1)} %param.9) | copy-start | bytes 73732
  425.7 119.1 %all-to-all-start.3 = ((bf16[2,8,192,768]{3,2,0,1:T(8,128)(2,1)}), bf16[2,8,192,768]{3,2,0,1:T(8,128)(2,1)}, u32[]{:S(2)}, u32[]{:S(2)}) async-start(bf16[2,8,192,768]{3,2,0,1:T(8,128)(2,1)} %copy.23), calls=%async_computation.3 | async-start | bytes 9437184 | tf_op jit(solution)/shard_map/all_to_all | solution.py:37
  836.8 18.4 %copy-start.1 = (f32[2,3072,768]{2,1,0:T(8,128)S(1)}, f32[2,3072,768]{2,1,0:T(8,128)}, u32[]{:S(2)}) copy-start(f32[2,3072,768]{2,1,0:T(8,128)} %get-tuple-element.35) | copy-start | bytes 56623108
Sparse Core Ops, SparseCore 0:
  402.4 434.3 all-reduce.2
where the time goes:
time: 877 us; the launch traced here: 869 us
  waiting for transfers between devices  321 us (37%)
  blocking collectives  231 us (26%)
  matrix products  171 us (19%)
  local copies, waits for them, and re-layouts  89.4 us (10%)
  other arithmetic  29.7 us (3%)
  between operations  14.5 us (2%)
  starting transfers between devices  11.6 us (1%)
    psum x1, waiting for transfers between devices, local_step(): grad_up = lax.psum(grad_up, 'dp')  284 us
    all_to_all x2, blocking collectives, dispatch(): return lax.all_to_all(picked, 'ep', 0, 0, tiled=True)  118 us
    psum x1, blocking collectives, local_step(): grad_gate = lax.psum(grad_gate, ('dp', 'ep'))  113 us
    dot_general x1, matrix products, local_step(): jnp.einsum('sekd,efd->eskf', recv_grad, w_down, preferred_element_type=jn...  43.6 us
    all_to_all x2, waiting for transfers between devices, combine(): returned = lax.all_to_all(expert_rows, 'ep', 1, 0, tiled=True)  37.1 us
    dot_general x1, matrix products, local_step(): jnp.einsum('eskf,sekd->efd', hidden, recv_grad, preferred_element_type=jn...  32.9 us
    unnamed x42, local copies, waits for them, and re-layouts  28.6 us
    gather x2, local copies, waits for them, and re-layouts, dispatch(): tok_rows[src_tok]  27.1 us
  transfers between devices with their start and end apart: 3, of which 2 were waited for; matrix products, arithmetic and copies ran while one was open for 5% of the time, Pallas kernels for 0%

commit v1 on v0

v1 whole, which is shorter than its diff:
```python
import functools
import jax
import jax.numpy as jnp
from jax import lax
from jax.experimental import pallas as pl
from jax.experimental.pallas import tpu as pltpu
from jax.sharding import PartitionSpec as P

ROWS = 256
F_TILE = 512
PAD_FACTOR = 4
BF = jnp.bfloat16
F32 = jnp.float32
SQRT_2_OVER_PI = 0.7978845608028654
NT = (((1,), (1,)), ((), ()))
TN = (((0,), (0,)), ((), ()))
MIB = 1024 * 1024


def dot(a, b, dims=(((1,), (0,)), ((), ()))):
    return lax.dot_general(a, b, dims, preferred_element_type=F32)


def iota(shape, dim):
    return lax.broadcasted_iota(jnp.int32, shape, dim)


def route_kernel(cap, first_ref, idx_ref, own_ref, pos_ref, off_ref, slot_ref):
    n_src, tok = idx_ref.shape
    n_experts = own_ref.shape[0]
    first = first_ref[0]
    before = (iota((tok, tok), 0) < iota((tok, tok), 1)).astype(BF)
    idx = idx_ref[...]
    pos = jnp.full((n_src, tok), -1.0, F32)
    base = jnp.zeros((1, 1), F32)
    lane = iota((8, 128), 1)
    sub = iota((8, 128), 0)
    off = jnp.zeros((8, 128), F32)
    for j in range(2):
        hit = idx == first + j
        rank = dot(hit.astype(BF), before)
        count = jnp.sum(hit.astype(F32), axis=1, keepdims=True)
        start = base
        starts = []
        for s in range(n_src):
            starts.append(start)
            off = jnp.where((sub == j) & (lane == s), start, off)
            start = start + count[s:s + 1, :]
        off = jnp.where((sub == j) & (lane == n_src), start, off)
        pos = jnp.where(hit, jnp.concatenate(starts, axis=0) + rank, pos)
        tiles = jnp.maximum(jnp.floor((start - base + (ROWS - 1)) * (1.0 / ROWS)), 1.0)
        base = base + tiles * ROWS
        off = jnp.where((sub == 2) & (lane == j), base * (1.0 / ROWS), off)
    pos_ref[...] = pos.astype(jnp.int32)
    off_ref[...] = off.astype(jnp.int32)
    own = own_ref[...] == iota(own_ref.shape, 0)
    own_rank = dot(own.astype(BF), before)
    row = iota(own.shape, 0).astype(F32) * cap + own_rank
    slot_ref[...] = jnp.sum(jnp.where(own, row, 0.0), axis=0, keepdims=True).astype(jnp.int32)


def route(first, idx_all, idx_own, n_experts, cap):
    n_src, tok = idx_all.shape
    vm = pl.BlockSpec(memory_space=pltpu.VMEM)
    return pl.pallas_call(
        functools.partial(route_kernel, cap),
        in_specs=[pl.BlockSpec(memory_space=pltpu.SMEM), vm, vm],
        out_specs=[vm, vm, vm],
        out_shape=[
            jax.ShapeDtypeStruct((n_src, tok), jnp.int32),
            jax.ShapeDtypeStruct((8, 128), jnp.int32),
            jax.ShapeDtypeStruct((1, tok), jnp.int32),
        ],
        cost_estimate=pl.CostEstimate(flops=10**8, bytes_accessed=10**5, transcendentals=0),
        name="route",
    )(first, idx_all, jnp.broadcast_to(idx_own[None, :], (n_experts, tok)))


def gate_of(x, wg, expert):
    n_experts = wg.shape[1]
    logit = dot(x, wg)
    ex = jnp.exp(logit - jnp.max(logit, axis=1, keepdims=True))
    prob = ex / jnp.sum(ex, axis=1, keepdims=True)
    mine = iota(prob.shape, 1) == expert
    gate = n_experts * jnp.sum(jnp.where(mine, prob, 0.0), axis=1, keepdims=True)
    return prob, mine, gate


def grad_kernel(off_ref, pos_ref, x_all, gy_all, wg_ref, w1_ref, w2_ref, x_ref, gy_ref, h_ref, da_ref, d1_ref, d2_ref, x_acc, g_acc):
    step = pl.program_id(0)
    n_src = pos_ref.shape[0]
    tok = pos_ref.shape[1]
    d_ff = w1_ref.shape[2]
    local = jnp.where(step >= off_ref[2, 0], 1, 0)
    row0 = step * ROWS

    @pl.when((step == 0) | (step == off_ref[2, 0]))
    def _():
        def clear(f, carry):
            cols = pl.ds(pl.multiple_of(f * F_TILE, F_TILE), F_TILE)
            d1_ref[0, :, cols] = jnp.zeros((d1_ref.shape[1], F_TILE), F32)
            d2_ref[0, cols, :] = jnp.zeros((F_TILE, d2_ref.shape[2]), F32)
            return carry

        lax.fori_loop(0, d_ff // F_TILE, clear, 0)

    @pl.when(step < off_ref[2, 1])
    def _():
        x_acc[...] = jnp.zeros_like(x_acc)
        g_acc[...] = jnp.zeros_like(g_acc)
        for s in range(n_src):
            @pl.when((off_ref[local, s] < row0 + ROWS) & (off_ref[local, s + 1] > row0))
            def _():
                pick = (iota((ROWS, tok), 0) + row0 == pos_ref[s:s + 1, :]).astype(BF)
                rows = slice(s * tok, (s + 1) * tok)
                x_acc[...] += dot(pick, x_all[rows, :])
                g_acc[...] += dot(pick, gy_all[rows, :])
        x = x_acc[...].astype(BF)
        gy = g_acc[...]
        x_ref[...] = x
        gy_ref[...] = gy.astype(BF)
        _, _, gate = gate_of(x, wg_ref[...], off_ref[2, 2] + local)
        dy = (gate * gy).astype(BF)

        def f_step(f, carry):
            cols = pl.ds(pl.multiple_of(f * F_TILE, F_TILE), F_TILE)
            a = dot(x, w1_ref[0, :, cols])
            dh = dot(dy, w2_ref[0, cols, :], NT)
            a2 = a * a
            t = jnp.tanh(SQRT_2_OVER_PI * (a + 0.044715 * (a2 * a)))
            cdf = 0.5 * (1.0 + t)
            h = (a * cdf).astype(BF)
            slope = cdf + a * (0.5 * (1.0 - t * t)) * (SQRT_2_OVER_PI * (1.0 + (3 * 0.044715) * a2))
            da = (slope * dh).astype(BF)
            h_ref[:, cols] = h
            da_ref[:, cols] = da
            d2_ref[0, cols, :] += dot(h, dy, TN)
            d1_ref[0, :, cols] += dot(x, da, TN)
            return carry

        lax.fori_loop(0, d_ff // F_TILE, f_step, 0)


def rows_kernel(off_ref, x_ref, gy_ref, h_ref, da_ref, wg_ref, w1_ref, w2_ref, out_ref, dx_ref, dwg_ref):
    step = pl.program_id(0)

    @pl.when(step == 0)
    def _():
        dwg_ref[...] = jnp.zeros_like(dwg_ref)

    @pl.when(step < off_ref[2, 1])
    def _():
        local = jnp.where(step >= off_ref[2, 0], 1, 0)
        x = x_ref[...]
        gy = gy_ref[...].astype(F32)
        prob, mine, gate = gate_of(x, wg_ref[...], off_ref[2, 2] + local)
        y = dot(h_ref[...], w2_ref[0]).astype(BF).astype(F32)
        dxe = dot(da_ref[...], w1_ref[0], NT).astype(BF).astype(F32)
        out_ref[...] = (gate * y).astype(BF)
        d_gate = jnp.sum(gy * y, axis=1, keepdims=True)
        dz = ((d_gate * gate) * (jnp.where(mine, 1.0, 0.0) - prob)).astype(BF)
        dwg_ref[...] += dot(x, dz, TN)
        dx_ref[...] = (dxe + dot(dz, wg_ref[...], NT)).astype(BF)


def tile_map(i, off_ref):
    return (jnp.minimum(i, off_ref[2, 1] - 1), 0)


def expert_map(i, off_ref):
    return (jnp.where(i >= off_ref[2, 0], 1, 0), 0, 0)


def whole(i, off_ref):
    return (0, 0)


def one_buffer(shape, index_map):
    return pl.BlockSpec(shape, index_map, pipeline_mode=pl.Buffered(1))


def grad_pass(off, pos, x_all, gy_all, w_gate, w_up, w_down, cap_rows):
    d_model, d_ff = w_up.shape[1:]
    up_block, down_block = (1, d_model, d_ff), (1, d_ff, d_model)
    row_spec = pl.BlockSpec((ROWS, d_model), tile_map)
    hid_spec = pl.BlockSpec((ROWS, d_ff), tile_map)
    sds = jax.ShapeDtypeStruct
    return pl.pallas_call(
        grad_kernel,
        grid_spec=pltpu.PrefetchScalarGridSpec(
            num_scalar_prefetch=1,
            grid=(cap_rows // ROWS,),
            in_specs=[
                one_buffer(pos.shape, whole), one_buffer(x_all.shape, whole), one_buffer(gy_all.shape, whole),
                one_buffer(w_gate.shape, whole), one_buffer(up_block, expert_map), one_buffer(down_block, expert_map)],
            out_specs=[
                row_spec, row_spec, hid_spec, hid_spec,
                one_buffer(up_block, expert_map), one_buffer(down_block, expert_map)],
            scratch_shapes=[pltpu.VMEM((ROWS, d_model), F32), pltpu.VMEM((ROWS, d_model), F32)],
        ),
        out_shape=[
            sds((cap_rows, d_model), BF), sds((cap_rows, d_model), BF), sds((cap_rows, d_ff), BF), sds((cap_rows, d_ff), BF),
            sds(w_up.shape, F32), sds(w_down.shape, F32)],
        compiler_params=pltpu.CompilerParams(vmem_limit_bytes=63 * MIB),
        cost_estimate=pl.CostEstimate(flops=4 * 10**10, bytes_accessed=60 * MIB, transcendentals=0),
        name="grad_pass",
    )(off, pos, x_all, gy_all, w_gate, w_up, w_down)


def rows_pass(off, x_rows, gy_rows, h, da, w_gate, w_up, w_down):
    d_model, d_ff = w_up.shape[1:]
    cap_rows = x_rows.shape[0]
    row_spec = pl.BlockSpec((ROWS, d_model), tile_map)
    hid_spec = pl.BlockSpec((ROWS, d_ff), tile_map)
    sds = jax.ShapeDtypeStruct
    return pl.pallas_call(
        rows_kernel,
        grid_spec=pltpu.PrefetchScalarGridSpec(
            num_scalar_prefetch=1,
            grid=(cap_rows // ROWS,),
            in_specs=[
                row_spec, row_spec, hid_spec, hid_spec, one_buffer(w_gate.shape, whole),
                one_buffer((1, d_model, d_ff), expert_map), one_buffer((1, d_ff, d_model), expert_map)],
            out_specs=[row_spec, row_spec, one_buffer(w_gate.shape, whole)],
        ),
        out_shape=[sds(x_rows.shape, BF), sds(x_rows.shape, BF), sds(w_gate.shape, F32)],
        compiler_params=pltpu.CompilerParams(vmem_limit_bytes=48 * MIB),
        cost_estimate=pl.CostEstimate(flops=2 * 10**10, bytes_accessed=40 * MIB, transcendentals=0),
        name="rows_pass",
    )(off, x_rows, gy_rows, h, da, w_gate, w_up, w_down)


def local_step(x, gy, idx, w_gate, w_up, w_down):
    tok, d_model = x.shape
    n_experts = w_gate.shape[1]
    n_local = w_up.shape[0]
    ep = lax.axis_size('ep')
    me = lax.axis_index('ep')
    cap = PAD_FACTOR * tok // n_experts
    cap_rows = n_local * -(-ep * cap // ROWS) * ROWS

    x_all = lax.all_gather(x, 'ep', tiled=True)
    gy_all = lax.all_gather(gy, 'ep', tiled=True)
    idx_all = lax.all_gather(idx, 'ep', tiled=True).reshape(ep, tok)
    first = (me * n_local).astype(jnp.int32)
    pos, off, slot = route(first.reshape(1), idx_all, idx, n_experts, cap)
    off = off[:4, :16]
    off = lax.dynamic_update_slice(off, first.reshape(1, 1), (2, 2))

    x_rows, gy_rows, h, da, d1, d2 = grad_pass(off, pos, x_all, gy_all, w_gate, w_up, w_down, cap_rows)
    grad_up, grad_down = lax.psum((d1, d2), 'dp')
    out_rows, dx_rows, dwg = rows_pass(off, x_rows, gy_rows, h, da, w_gate, w_up, w_down)

    take = off[:n_local, :ep].T[:, :, None] + jnp.arange(cap, dtype=jnp.int32)[None, None, :]
    take = jnp.minimum(take.reshape(-1), cap_rows - 1)

    def back(rows):
        got = lax.all_to_all(rows[take].reshape(ep, n_local * cap, d_model), 'ep', 0, 0, tiled=True)
        return got.reshape(n_experts * cap, d_model)[slot.reshape(-1)]

    moe_out = back(out_rows)
    grad_x = back(dx_rows)
    grad_gate = lax.psum(dwg, ('dp', 'ep'))
    return moe_out, grad_x, grad_up, grad_down, grad_gate


def solution(mesh):
    tok_spec, exp_spec, rep = P(('dp', 'ep'), None), P('ep', None, None), P(None, None)
    return jax.shard_map(
        local_step, mesh=mesh,
        in_specs=(tok_spec, tok_spec, P(('dp', 'ep')), rep, exp_spec, exp_spec),
        out_specs=(tok_spec, tok_spec, exp_spec, exp_spec, rep),
        check_vma=False,
    )
```

time: 877 us -> 680 us (0.78)
  matrix products: 171 us -> 0 us
  Pallas kernels: 0 us -> 102 us
  blocking collectives: 231 us -> 148 us
  other arithmetic: 29.7 us -> 0.12 us
    dot_general x9 -> x0, matrix products: 171 us -> none  [the longest x1 43.6 us: local_step(): jnp.einsum('sekd,efd->eskf', recv_grad, w_down, preferred_element_type=jn...]
    all_to_all x2 -> x0, blocking collectives: 118 us -> none  [dispatch(): return lax.all_to_all(picked, 'ep', 0, 0, tiled=True)]
    pallas_call x0 -> x3, Pallas kernels: none -> 102 us  [the longest x1 76.8 us: grad_pass(): pl.pallas_call(grad_kernel, grid_spec=pltpu.PrefetchScalarGridSpec(num_sc...]
    psum x1, waiting for transfers between devices: 284 us -> 190 us  [local_step(): grad_up, grad_down = lax.psum((d1, d2), 'dp')]
    all_gather x0 -> x2, waiting for transfers between devices: none -> 93.2 us  [the longest x1 55.9 us: local_step(): gy_all = lax.all_gather(gy, 'ep', tiled=True)]
    psum x1, blocking collectives: 113 us -> 134 us  [local_step(): grad_gate = lax.psum(dwg, ('dp', 'ep'))]
    select_n x5 -> x2, other arithmetic: 15.5 us -> 0.03 us  [the longest x1 0.02 us: back(): return got.reshape(n_experts * cap, d_model)[slot.reshape(-1)]]
    all_gather x0 -> x1, blocking collectives: none -> 14.4 us  [local_step(): idx_all = lax.all_gather(idx, 'ep', tiled=True).reshape(ep, tok)]
  transfers between devices with their start and end apart: 3 -> 5, of which waited for: 2 -> 4; matrix products, arithmetic and copies ran while one was open for 5% -> 8% of each run, Pallas kernels for 0% -> 4%
where the time goes in v1:
time: 680 us; the launch traced here: 679 us
  waiting for transfers between devices  322 us (47%)
  blocking collectives  148 us (22%)
  Pallas kernels  102 us (15%)
  local copies, waits for them, and re-layouts  82.8 us (12%)
  between operations  13.8 us (2%)
  starting transfers between devices  10.6 us (2%)
    psum x1, waiting for transfers between devices, local_step(): grad_up, grad_down = lax.psum((d1, d2), 'dp')  190 us
    psum x1, blocking collectives, local_step(): grad_gate = lax.psum(dwg, ('dp', 'ep'))  134 us
    pallas_call x1, Pallas kernels, grad_pass(): pl.pallas_call(grad_kernel, grid_spec=pltpu.PrefetchScalarGridSpec(num_sc...  76.8 us
    all_gather x1, waiting for transfers between devices, local_step(): gy_all = lax.all_gather(gy, 'ep', tiled=True)  55.9 us
    all_gather x1, waiting for transfers between devices, local_step(): x_all = lax.all_gather(x, 'ep', tiled=True)  37.3 us
    all_to_all x2, waiting for transfers between devices, back(): lax.all_to_all(rows[take].reshape(ep, n_local * cap, d_model), 'ep', 0, 0...  36.7 us
    gather x2, local copies, waits for them, and re-layouts, back(): rows[take].reshape(ep, n_local * cap, d_model)  35 us
    unnamed x18, local copies, waits for them, and re-layouts  31.7 us
  transfers between devices with their start and end apart: 5, of which 4 were waited for; matrix products, arithmetic and copies ran while one was open for 8% of the time, Pallas kernels for 4%

profile of v1, /device:TPU:1, one launch (start us, length us, event | category | flops | bytes accessed | tf_op | source)
XLA Modules:
  0.0 679.2 jit_solution(17377447882122896907)
XLA Ops:
  7.2 0.0 all-gather.4.cloned.1.call-start
  7.2 0.7 all-gather.4.cloned.1.call-update
  7.9 0.0 all-gather.6.cloned.1.call-start
  7.9 0.7 all-gather.6.cloned.1.call-update
  8.6 0.0 all-reduce.3.cloned.1.call-start
  8.7 0.7 reshape.140
  9.4 14.4 %all-gather = s32[8,1,768]{2,1,0:T(1,128)S(1)} all-gather(s32[1,1,768]{2,1,0:T(1,128)S(1)} %reshape.140), channel_id=1, replica_groups=mesh['dp'=16,'ep'=8] {'ep'}, dimensions={0}, use_global_device_ids=true | all-gather | bytes 27648 | tf_op jit(solution)/shard_map/all_gather | solution.py:244
  23.8 0.6 copy.25
  24.4 1.3 broadcast_in_dim.2.own_ref
  25.7 1.9 route.1
  27.6 0.7 slice.6
  28.3 1.6 copy.19.wg_ref
  29.8 0.1 dynamic_update_slice.3.off_ref
  29.9 0.0 copy-start.2
  29.9 37.3 %all-gather.4.cloned.1.call-done.x_all = bf16[6144,768]{1,0:T(8,128)(2,1)} async-done(((bf16[768,768]{1,0:T(8,128)(2,1)}), bf16[6144,768]{1,0:T(8,128)(2,1)}) %all-gather.4.cloned.1.call-update) | async-done | bytes 9437200 | tf_op jit(solution)/shard_map/all_gather | solution.py:242
  67.2 55.9 %all-gather.6.cloned.1.call-done.gy_all = bf16[6144,768]{1,0:T(8,128)(2,1)} async-done(((bf16[768,768]{1,0:T(8,128)(2,1)}), bf16[6144,768]{1,0:T(8,128)(2,1)}) %all-gather.6.cloned.1.call-update) | async-done | bytes 9437200 | tf_op jit(solution)/shard_map/all_gather | solution.py:243
  123.2 0.0 copy-done.2
  123.2 76.8 %grad_pass.1 = (bf16[3072,768]{1,0:T(8,128)(2,1)}, bf16[3072,768]{1,0:T(8,128)(2,1)}, bf16[3072,3072]{1,0:T(8,128)(2,1)}, bf16[3072,3072]{1,0:T(8,128)(2,1)}, f3...) custom-call(s32[4,16]{1,0:T(4,128)} %copy-done.2, s32[8,768]{1,0:T(8,128)} %get-tuple-element.18.pos_ref, ...), custom_call_target="tpu_custom_call" | custom-call | flops 40000000000 | bytes 62914560 | tf_op jit(solution)/shard_map/grad_pass/pallas_call | solution.py:188
  199.9 0.0 copy-start.3
  200.0 0.0 copy-start.1
  200.0 0.0 all-reduce.3.cloned.1.call-update
  200.0 0.6 copy-done.3
  200.6 0.1 copy.21
  200.7 0.1 add_minimum_fusion
  200.8 0.1 min.18
  200.9 0.0 copy-done.1
  200.9 23.4 %rows_pass.1 = (bf16[3072,768]{1,0:T(8,128)(2,1)S(1)}, bf16[3072,768]{1,0:T(8,128)(2,1)}, f32[768,16]{1,0:T(8,128)S(1)}) custom-call(s32[4,16]{1,0:T(4,128)S(1)} %copy-done.3, bf16[3072,768]{1,0:T(8,128)(2,1)} %get-tuple-element.19.x_ref, bf16[3072,768]{1,0:T(8,128)(2,1)} %get-tuple-element.20.gy_ref, bf16[3072,3072]{1,0:T(8,128)(2,1)} %get-tuple-element.21.h_ref, ...), custom_call_target="tpu_custom_call" | custom-call | flops 20000000000 | bytes 41943040 | tf_op jit(solution)/shard_map/rows_pass/pallas_call | solution.py:216
  224.3 0.0 copy-start
  224.3 2.2 copy-done
  226.5 17.5 %gather_fusion.2 = bf16[3072,768]{1,0:T(8,128)(2,1)} fusion(bf16[3072,768]{1,0:T(8,128)(2,1)} %get-tuple-element.25, s32[3072]{0:T(1024)S(1)} %broadcast_clamp_fusion), kind=kCustom, calls=%fused_computation.2 | custom fusion | bytes 9449472 | tf_op jit(solution)/shard_map/gather | solution.py:258
  244.0 4.8 all-to-all-start.1
  248.8 17.5 %gather_fusion = bf16[3072,768]{1,0:T(8,128)(2,1)} fusion(bf16[3072,768]{1,0:T(8,128)(2,1)} %copy-done, s32[3072]{0:T(1024)S(1)} %broadcast_clamp_fusion), kind=kCustom, calls=%fused_computation | custom fusion | bytes 9449472 | tf_op jit(solution)/shard_map/gather | solution.py:258
  266.3 36.7 %all-to-all-done.1 = bf16[8,384,768]{2,1,0:T(8,128)(2,1)} async-done(((bf16[8,384,768]{2,1,0:T(8,128)(2,1)}), bf16[8,384,768]{2,1,0:T(8,128)(2,1)}, u32[]{:S(2)}, u32[]{:S(2)}) %all-to-all-start.1) | async-done | bytes 4718624 | tf_op jit(solution)/shard_map/all_to_all | solution.py:258
  303.0 0.0 copy-start.5
  303.0 5.7 all-to-all-start
  308.7 0.0 copy-done.5
  308.8 133.7 %psum.23 = f32[768,16]{1,0:T(8,128)S(1)} all-reduce(f32[768,16]{1,0:T(8,128)S(1)} %get-tuple-element.28), channel_id=1, replica_groups=mesh['dp'=16,'ep'=8] {'dp','ep'}, use_global_device_ids=true, to_apply=%region_2.0 | all-reduce | flops 12288 | bytes 98304 | tf_op jit(solution)/shard_map/psum | solution.py:263
  442.5 0.8 copy.22
  443.2 6.9 %gather_fusion.3 = bf16[768,768]{1,0:T(8,128)(2,1)} fusion(bf16[3072,768]{1,0:T(8,128)(2,1)} %bitcast.8, s32[1024]{0:T(1024)S(1)} %pad_clamp_fusion), kind=kCustom, calls=%fused_computation.3 | custom fusion | bytes 2362368 | tf_op jit(solution)/shard_map/gather | solution.py:259
  450.1 0.0 all-to-all-done
  450.1 6.9 %gather_fusion.1 = bf16[768,768]{1,0:T(8,128)(2,1)} fusion(bf16[3072,768]{1,0:T(8,128)(2,1)} %bitcast.5, s32[1024]{0:T(1024)S(1)} %pad_clamp_fusion), kind=kCustom, calls=%fused_computation.1 | custom fusion | bytes 2362368 | tf_op jit(solution)/shard_map/gather | solution.py:259
  457.1 190.4 %all-reduce.3.cloned.1.call-done = (f32[2,768,3072]{2,1,0:T(8,128)}, f32[2,3072,768]{2,1,0:T(8,128)}) async-done(((f32[2,768,3072]{2,1,0:T(8,128)}, f32[2,3072,768]{2,1,0:T(8,128)}), (f32[2,768,3072]{2,1,0:T(8,128)}, f32[2,3072,768]{2,1,0:T(8,128)})) %all-reduce.3.cloned.1.call-update) | async-done | bytes 37748752 | tf_op jit(solution)/shard_map/psum | solution.py:251
  647.5 0.0 copy-start.4
  647.5 14.0 %copy.29 = f32[2,768,3072]{2,1,0:T(8,128)} copy(f32[2,768,3072]{2,1,0:T(8,128)} %get-tuple-element.48) | data formatting | bytes 37748736
  661.4 4.4 copy-done.4
  665.8 6.8 %copy.30 = f32[2,3072,768]{2,1,0:T(8,128)} copy(f32[2,3072,768]{2,1,0:T(8,128)S(1)} %copy-done.4) | data formatting | bytes 37748736
  (5 shorter events, 0.0 us)
Async XLA Ops:
  7.2 60.0 %all-gather.4.cloned.1.call-start = ((), (), s32[]{:S(2)}) async-start(), calls=%async_computation.2 | async-start | bytes 10616832 | tf_op jit(solution)/shard_map/all_gather | solution.py:242
  7.9 115.3 %all-gather.6.cloned.1.call-start = ((), (), s32[]{:S(2)}) async-start(), calls=%async_computation.3 | async-start | bytes 10616832 | tf_op jit(solution)/shard_map/all_gather | solution.py:243
  8.6 638.8 %all-reduce.3.cloned.1.call-start = ((), (), s32[]{:S(2)}) async-start(), calls=%async_computation.4 | async-start | bytes 75497472 | tf_op jit(solution)/shard_map/psum | solution.py:251
  29.9 93.2 %copy-start.2 = (s32[4,16]{1,0:T(4,128)}, s32[4,16]{1,0:T(4,128)S(1)}, u32[]{:S(2)}) copy-start(s32[4,16]{1,0:T(4,128)S(1)} %dynamic_update_slice.3.off_ref) | copy-start | bytes 772
  199.9 0.7 copy-start.3
  200.0 1.0 copy-start.1
  224.3 2.2 copy-start
  244.0 59.0 %all-to-all-start.1 = ((bf16[8,384,768]{2,1,0:T(8,128)(2,1)}), bf16[8,384,768]{2,1,0:T(8,128)(2,1)}, u32[]{:S(2)}, u32[]{:S(2)}) async-start(bf16[8,384,768]{2,1,0:T(8,128)(2,1)} %bitcast.15), calls=%async_computation.1 | async-start | bytes 9437184 | tf_op jit(solution)/shard_map/all_to_all | solution.py:258
  303.0 5.7 copy-start.5
  303.0 147.1 %all-to-all-start = ((bf16[8,384,768]{2,1,0:T(8,128)(2,1)}), bf16[8,384,768]{2,1,0:T(8,128)(2,1)}, u32[]{:S(2)}, u32[]{:S(2)}) async-start(bf16[8,384,768]{2,1,0:T(8,128)(2,1)} %bitcast.14), calls=%async_computation | async-start | bytes 9437184 | tf_op jit(solution)/shard_map/all_to_all | solution.py:258
  647.5 18.4 %copy-start.4 = (f32[2,3072,768]{2,1,0:T(8,128)S(1)}, f32[2,3072,768]{2,1,0:T(8,128)}, u32[]{:S(2)}) copy-start(f32[2,3072,768]{2,1,0:T(8,128)} %get-tuple-element.49) | copy-start | bytes 56623108
Sparse Core Ops, SparseCore 0:
  9.7 57.5 all-gather.3
  68.9 54.2 all-gather.5
  200.1 447.3 all-reduce.2

commit v2 on v1

--- a/solution.py
+++ b/solution.py
@@ -6,8 +6,9 @@
 from jax.experimental.pallas import tpu as pltpu
 from jax.sharding import PartitionSpec as P
 
-ROWS = 256
-F_TILE = 512
+ROWS = 512
+PICK = 128
+F_TILE = 1024
 PAD_FACTOR = 4
 BF = jnp.bfloat16
 F32 = jnp.float32
@@ -86,59 +87,89 @@
     return prob, mine, gate
 
 
-def grad_kernel(off_ref, pos_ref, x_all, gy_all, wg_ref, w1_ref, w2_ref, x_ref, gy_ref, h_ref, da_ref, d1_ref, d2_ref, x_acc, g_acc):
+def pick_kernel(off_ref, pos_ref, x_all, gy_all, x_ref, gy_ref, x_acc, g_acc):
     step = pl.program_id(0)
-    n_src = pos_ref.shape[0]
-    tok = pos_ref.shape[1]
-    d_ff = w1_ref.shape[2]
-    local = jnp.where(step >= off_ref[2, 0], 1, 0)
-    row0 = step * ROWS
-
-    @pl.when((step == 0) | (step == off_ref[2, 0]))
-    def _():
-        def clear(f, carry):
-            cols = pl.ds(pl.multiple_of(f * F_TILE, F_TILE), F_TILE)
-            d1_ref[0, :, cols] = jnp.zeros((d1_ref.shape[1], F_TILE), F32)
-            d2_ref[0, cols, :] = jnp.zeros((F_TILE, d2_ref.shape[2]), F32)
-            return carry
-
-        lax.fori_loop(0, d_ff // F_TILE, clear, 0)
-
-    @pl.when(step < off_ref[2, 1])
+    n_src, tok = pos_ref.shape
+    per = ROWS // PICK
+    local = jnp.where(step >= off_ref[2, 0] * per, 1, 0)
+    row0 = step * PICK
+
+    @pl.when(step < off_ref[2, 1] * per)
     def _():
         x_acc[...] = jnp.zeros_like(x_acc)
         g_acc[...] = jnp.zeros_like(g_acc)
         for s in range(n_src):
-            @pl.when((off_ref[local, s] < row0 + ROWS) & (off_ref[local, s + 1] > row0))
+            @pl.when((off_ref[local, s] < row0 + PICK) & (off_ref[local, s + 1] > row0))
             def _():
-                pick = (iota((ROWS, tok), 0) + row0 == pos_ref[s:s + 1, :]).astype(BF)
-                rows = slice(s * tok, (s + 1) * tok)
-                x_acc[...] += dot(pick, x_all[rows, :])
-                g_acc[...] += dot(pick, gy_all[rows, :])
-        x = x_acc[...].astype(BF)
-        gy = g_acc[...]
-        x_ref[...] = x
-        gy_ref[...] = gy.astype(BF)
+                pick = (iota((PICK, tok), 0) + row0 == pos_ref[s:s + 1, :]).astype(BF)
+                x_acc[...] += dot(pick, x_all[s])
+                g_acc[...] += dot(pick, gy_all[s])
+        x_ref[...] = x_acc[...].astype(BF)
+        gy_ref[...] = g_acc[...].astype(BF)
+
+
+def grad_kernel(off_ref, x_ref, gy_ref, wg_ref, w1_ref, w2_ref, h_ref, da_ref, d1_out, d2_out, xt_ref, d1_acc, d2_acc, sem):
+    step = pl.program_id(0)
+    n_f = w1_ref.shape[2] // F_TILE
+    total = off_ref[2, 1]
+    split = off_ref[2, 0]
+    local = jnp.where(step >= split, 1, 0)
+    first = (step == 0) | (step == split)
+    last = (step == split - 1) | (step == total - 1)
+
+    def flush(f, which):
+        cols = pl.ds(pl.multiple_of(f * F_TILE, F_TILE), F_TILE)
+        return (
+            pltpu.make_async_copy(d1_acc.at[:, cols], d1_out.at[which, :, cols], sem.at[0, f]),
+            pltpu.make_async_copy(d2_acc.at[cols, :], d2_out.at[which, cols, :], sem.at[1, f]))
+
+    def finish(f, which):
+        for c in flush(f, which):
+            c.wait()
+
+    @pl.when(step < total)
+    def _():
+        x = x_ref[...]
+        xt_ref[...] = x.T
         _, _, gate = gate_of(x, wg_ref[...], off_ref[2, 2] + local)
-        dy = (gate * gy).astype(BF)
+        dy = (gate * gy_ref[...].astype(F32)).astype(BF)
 
         def f_step(f, carry):
             cols = pl.ds(pl.multiple_of(f * F_TILE, F_TILE), F_TILE)
             a = dot(x, w1_ref[0, :, cols])
             dh = dot(dy, w2_ref[0, cols, :], NT)
             a2 = a * a
-            t = jnp.tanh(SQRT_2_OVER_PI * (a + 0.044715 * (a2 * a)))
-            cdf = 0.5 * (1.0 + t)
+            t = jnp.tanh(a * (SQRT_2_OVER_PI + (SQRT_2_OVER_PI * 0.044715) * a2))
+            cdf = 0.5 + 0.5 * t
             h = (a * cdf).astype(BF)
-            slope = cdf + a * (0.5 * (1.0 - t * t)) * (SQRT_2_OVER_PI * (1.0 + (3 * 0.044715) * a2))
+            slope = cdf + (0.5 * a) * (1.0 - t * t) * (SQRT_2_OVER_PI + (SQRT_2_OVER_PI * 3 * 0.044715) * a2)
             da = (slope * dh).astype(BF)
             h_ref[:, cols] = h
             da_ref[:, cols] = da
-            d2_ref[0, cols, :] += dot(h, dy, TN)
-            d1_ref[0, :, cols] += dot(x, da, TN)
+
+            @pl.when(step == split)
+            def _():
+                finish(f, 0)
+
+            d2_acc[cols, :] = jnp.where(first, 0.0, d2_acc[cols, :]) + dot(h, dy, TN)
+            d1_acc[:, cols] = jnp.where(first, 0.0, d1_acc[:, cols]) + dot(xt_ref[...], da)
+
+            @pl.when(last)
+            def _():
+                for c in flush(f, local):
+                    c.start()
+
             return carry
 
-        lax.fori_loop(0, d_ff // F_TILE, f_step, 0)
+        lax.fori_loop(0, n_f, f_step, 0)
+
+    @pl.when(step == total - 1)
+    def _():
+        def drain(f, carry):
+            finish(f, 1)
+            return carry
+
+        lax.fori_loop(0, n_f, drain, 0)
 
 
 def rows_kernel(off_ref, x_ref, gy_ref, h_ref, da_ref, wg_ref, w1_ref, w2_ref, out_ref, dx_ref, dwg_ref):
@@ -179,11 +210,148 @@
     return pl.BlockSpec(shape, index_map, pipeline_mode=pl.Buffered(1))
 
 
-def grad_pass(off, pos, x_all, gy_all, w_gate, w_up, w_down, cap_rows):
+def gather_kernel(x_in, gy_in, idx_in, x_all, gy_all, idx_all, x_buf, gy_buf, send_r, send_l, send_p, recv_l, recv_r, recv_p, own_sem):
+    n_x = lax.axis_size('ep') // 2
+    me = lax.axis_index('ep')
+    chip, core = me // 2, me % 2
+    left = (chip + n_x - 1) % n_x * 2 + core
+    right = (chip + 1) % n_x * 2 + core
+    far = (chip + 2) % n_x * 2 + core
+    partner = chip * 2 + 1 - core
+
+    barrier = pltpu.get_barrier_semaphore()
+    for peer in (left, right, partner):
+        pl.semaphore_signal(barrier, inc=1, device_id={'ep': peer}, device_id_type=pl.DeviceIdType.MESH)
+    pl.semaphore_wait(barrier, 3)
+
+    half = x_in.shape[0] // 2
+    top, bottom = pl.ds(0, half), pl.ds(half, half)
+    pieces = [(idx_in, idx_all, None), (x_in, x_all, top), (gy_in, gy_all, top), (x_in, x_all, bottom), (gy_in, gy_all, bottom)]
+    n_piece = len(pieces)
+    to_right = (0, 1, 2)
+    to_left = (3, 4)
+    order_right = (0, 1, 3, 2, 4)
+    order_left = (0, 3, 1, 4, 2)
+
+    def at(ref, owner, rows):
+        return ref.at[owner] if rows is None else ref.at[owner, rows]
+
+    def copy(k, owner, source, send_sem, recv_sem, peer):
+        src, dst, rows = pieces[k]
+        if source is None:
+            src = src if rows is None else src.at[rows]
+        else:
+            src = at(dst, source, rows)
+        return pltpu.make_async_remote_copy(
+            src_ref=src, dst_ref=at(dst, owner, rows), send_sem=send_sem, recv_sem=recv_sem,
+            device_id={'ep': peer}, device_id_type=pl.DeviceIdType.MESH)
+
+    right_own = [copy(k, me, None, send_r.at[k], recv_l.at[k], right) for k in range(n_piece)]
+    left_own = [copy(k, me, None, send_l.at[k], recv_r.at[k], left) for k in range(n_piece)]
+    part_own = [copy(k, me, None, send_p.at[k], recv_p.at[k], partner) for k in range(n_piece)]
+    for a, b in zip(order_right, order_left):
+        right_own[a].start()
+        left_own[b].start()
+    for c in part_own:
+        c.start()
+
+    own = [
+        pltpu.make_async_copy(x_in, x_buf, own_sem.at[0]), pltpu.make_async_copy(gy_in, gy_buf, own_sem.at[1]),
+        pltpu.make_async_copy(x_buf, x_all.at[me], own_sem.at[2]), pltpu.make_async_copy(gy_buf, gy_all.at[me], own_sem.at[3]),
+        pltpu.make_async_copy(idx_in, idx_all.at[me], own_sem.at[4])]
+    own[0].start()
+    own[1].start()
+    own[4].start()
+    own[0].wait()
+    own[2].start()
+    own[1].wait()
+    own[3].start()
+
+    def part(k, owner, group):
+        return copy(k, owner, owner, send_p.at[group * n_piece + k], recv_p.at[group * n_piece + k], partner)
+
+    forward = {}
+    part_fwd = []
+    for a, b in zip(order_right, order_left):
+        right_own[a].wait_recv()
+        if a in to_right:
+            forward[a] = copy(a, left, left, send_r.at[n_piece + a], recv_l.at[n_piece + a], right)
+            forward[a].start()
+        part_fwd.append(part(a, left, 1))
+        part_fwd[-1].start()
+        left_own[b].wait_recv()
+        if b in to_left:
+            forward[b] = copy(b, right, right, send_l.at[n_piece + b], recv_r.at[n_piece + b], left)
+            forward[b].start()
+        part_fwd.append(part(b, right, 2))
+        part_fwd[-1].start()
+    for k in (0, 1, 3, 2, 4):
+        forward[k].wait_recv()
+        part_fwd.append(part(k, far, 3))
+        part_fwd[-1].start()
+    for c in part_own + part_fwd:
+        c.wait_recv()
+    for c in right_own + left_own + part_own + part_fwd + list(forward.values()):
+        c.wait_send()
+    own[2].wait()
+    own[3].wait()
+    own[4].wait()
+
+
+def gather_rows(x, gy, idx):
+    n = lax.axis_size('ep')
+    anywhere = pl.BlockSpec(memory_space=pl.ANY)
+    sem = pltpu.SemaphoreType.DMA
+    sds = jax.ShapeDtypeStruct
+    return pl.pallas_call(
+        gather_kernel,
+        in_specs=[anywhere] * 3,
+        out_specs=[anywhere] * 3,
+        out_shape=[sds((n,) + x.shape, x.dtype), sds((n,) + gy.shape, gy.dtype), sds((n,) + idx.shape, idx.dtype)],
+        scratch_shapes=[
+            pltpu.VMEM(x.shape, x.dtype), pltpu.VMEM(gy.shape, gy.dtype),
+            sem((10,)), sem((10,)), sem((20,)), sem((10,)), sem((10,)), sem((20,)), sem((5,))],
+        compiler_params=pltpu.CompilerParams(collective_id=0, has_side_effects=True),
+        cost_estimate=pl.CostEstimate(flops=8 * 10**10, bytes_accessed=60 * MIB, transcendentals=0),
+        name="gather_rows",
+    )(x, gy, idx)
+
+
+def pick_pass(off, pos, x_all, gy_all, cap_rows):
+    d_model = x_all.shape[2]
+    per = ROWS // PICK
+
+    def pick_map(i, off_ref):
+        return (jnp.minimum(i, off_ref[2, 1] * per - 1), 0)
+
+    def whole3(i, off_ref):
+        return (0, 0, 0)
+
+    spec = pl.BlockSpec((PICK, d_model), pick_map)
+    sds = jax.ShapeDtypeStruct
+    return pl.pallas_call(
+        pick_kernel,
+        grid_spec=pltpu.PrefetchScalarGridSpec(
+            num_scalar_prefetch=1,
+            grid=(cap_rows // PICK,),
+            in_specs=[one_buffer(pos.shape, whole), one_buffer(x_all.shape, whole3), one_buffer(gy_all.shape, whole3)],
+            out_specs=[spec, spec],
+            scratch_shapes=[pltpu.VMEM((PICK, d_model), F32), pltpu.VMEM((PICK, d_model), F32)],
+        ),
+        out_shape=[sds((cap_rows, d_model), BF), sds((cap_rows, d_model), BF)],
+        compiler_params=pltpu.CompilerParams(vmem_limit_bytes=40 * MIB),
+        cost_estimate=pl.CostEstimate(flops=10**10, bytes_accessed=20 * MIB, transcendentals=0),
+        name="pick_pass",
+    )(off, pos, x_all, gy_all)
+
+
+def grad_pass(off, x_rows, gy_rows, w_gate, w_up, w_down):
     d_model, d_ff = w_up.shape[1:]
+    cap_rows = x_rows.shape[0]
     up_block, down_block = (1, d_model, d_ff), (1, d_ff, d_model)
     row_spec = pl.BlockSpec((ROWS, d_model), tile_map)
     hid_spec = pl.BlockSpec((ROWS, d_ff), tile_map)
+    anywhere = pl.BlockSpec(memory_space=pl.ANY)
     sds = jax.ShapeDtypeStruct
     return pl.pallas_call(
         grad_kernel,
@@ -191,20 +359,18 @@
             num_scalar_prefetch=1,
             grid=(cap_rows // ROWS,),
             in_specs=[
-                one_buffer(pos.shape, whole), one_buffer(x_all.shape, whole), one_buffer(gy_all.shape, whole),
-                one_buffer(w_gate.shape, whole), one_buffer(up_block, expert_map), one_buffer(down_block, expert_map)],
-            out_specs=[
-                row_spec, row_spec, hid_spec, hid_spec,
-                one_buffer(up_block, expert_map), one_buffer(down_block, expert_map)],
-            scratch_shapes=[pltpu.VMEM((ROWS, d_model), F32), pltpu.VMEM((ROWS, d_model), F32)],
+                row_spec, row_spec, one_buffer(w_gate.shape, whole),
+                pl.BlockSpec(up_block, expert_map), pl.BlockSpec(down_block, expert_map)],
+            out_specs=[hid_spec, hid_spec, anywhere, anywhere],
+            scratch_shapes=[
+                pltpu.VMEM((d_model, ROWS), BF), pltpu.VMEM((d_model, d_ff), F32), pltpu.VMEM((d_ff, d_model), F32),
+                pltpu.SemaphoreType.DMA((2, d_ff // F_TILE))],
         ),
-        out_shape=[
-            sds((cap_rows, d_model), BF), sds((cap_rows, d_model), BF), sds((cap_rows, d_ff), BF), sds((cap_rows, d_ff), BF),
-            sds(w_up.shape, F32), sds(w_down.shape, F32)],
+        out_shape=[sds((cap_rows, d_ff), BF), sds((cap_rows, d_ff), BF), sds(w_up.shape, F32), sds(w_down.shape, F32)],
         compiler_params=pltpu.CompilerParams(vmem_limit_bytes=63 * MIB),
         cost_estimate=pl.CostEstimate(flops=4 * 10**10, bytes_accessed=60 * MIB, transcendentals=0),
         name="grad_pass",
-    )(off, pos, x_all, gy_all, w_gate, w_up, w_down)
+    )(off, x_rows, gy_rows, w_gate, w_up, w_down)
 
 
 def rows_pass(off, x_rows, gy_rows, h, da, w_gate, w_up, w_down):
@@ -239,15 +405,15 @@
     cap = PAD_FACTOR * tok // n_experts
     cap_rows = n_local * -(-ep * cap // ROWS) * ROWS
 
-    x_all = lax.all_gather(x, 'ep', tiled=True)
-    gy_all = lax.all_gather(gy, 'ep', tiled=True)
-    idx_all = lax.all_gather(idx, 'ep', tiled=True).reshape(ep, tok)
+    x_all, gy_all, idx_all = gather_rows(x, gy, idx.reshape(1, tok))
+    idx_all = idx_all.reshape(ep, tok)
     first = (me * n_local).astype(jnp.int32)
     pos, off, slot = route(first.reshape(1), idx_all, idx, n_experts, cap)
     off = off[:4, :16]
     off = lax.dynamic_update_slice(off, first.reshape(1, 1), (2, 2))
 
-    x_rows, gy_rows, h, da, d1, d2 = grad_pass(off, pos, x_all, gy_all, w_gate, w_up, w_down, cap_rows)
+    x_rows, gy_rows = pick_pass(off, pos, x_all, gy_all, cap_rows)
+    h, da, d1, d2 = grad_pass(off, x_rows, gy_rows, w_gate, w_up, w_down)
     grad_up, grad_down = lax.psum((d1, d2), 'dp')
     out_rows, dx_rows, dwg = rows_pass(off, x_rows, gy_rows, h, da, w_gate, w_up, w_down)
 

time: 680 us -> 643 us (0.946)
  waiting for transfers between devices: 322 us -> 219 us
  Pallas kernels: 102 us -> 185 us
  blocking collectives: 148 us -> 131 us
    pallas_call x0 -> x2, Pallas kernels: none -> 104 us  [the longest x1 84.7 us: gather_rows(): pl.pallas_call(gather_kernel, in_specs=[anywhere] * 3, out_specs=[anywher...]
    all_gather x2 -> x0, waiting for transfers between devices: 93.2 us -> none  [the longest x1 55.9 us: local_step(): gy_all = lax.all_gather(gy, 'ep', tiled=True)]
    pallas_call x1, Pallas kernels: 76.8 us -> 48.7 us  [grad_pass(): pl.pallas_call(grad_kernel, grid_spec=pltpu.PrefetchScalarGridSpec(num_sc...]
    all_gather x1 -> x0, blocking collectives: 14.4 us -> none  [local_step(): idx_all = lax.all_gather(idx, 'ep', tiled=True).reshape(ep, tok)]
    unnamed x18 -> x27, local copies, waits for them, and re-layouts: 31.7 us -> 36 us
  transfers between devices with their start and end apart: 5 -> 3, of which waited for: 4 -> 2; matrix products, arithmetic and copies ran while one was open for 8% -> 8% of each run, Pallas kernels for 4% -> 5%
where the time goes in v2:
time: 643 us; the launch traced here: 646 us
  waiting for transfers between devices  219 us (34%)
  Pallas kernels  185 us (29%)
  blocking collectives  131 us (20%)
  local copies, waits for them, and re-layouts  87.8 us (14%)
  between operations  14.2 us (2%)
  starting transfers between devices  10.3 us (2%)
    psum x1, waiting for transfers between devices, local_step(): grad_up, grad_down = lax.psum((d1, d2), 'dp')  184 us
    psum x1, blocking collectives, local_step(): grad_gate = lax.psum(dwg, ('dp', 'ep'))  131 us
    pallas_call x1, Pallas kernels, gather_rows(): pl.pallas_call(gather_kernel, in_specs=[anywhere] * 3, out_specs=[anywher...  84.7 us
    pallas_call x1, Pallas kernels, grad_pass(): pl.pallas_call(grad_kernel, grid_spec=pltpu.PrefetchScalarGridSpec(num_sc...  48.7 us
    unnamed x27, local copies, waits for them, and re-layouts  36 us
    all_to_all x2, waiting for transfers between devices, back(): lax.all_to_all(rows[take].reshape(ep, n_local * cap, d_model), 'ep', 0, 0...  35.1 us
    gather x2, local copies, waits for them, and re-layouts, back(): rows[take].reshape(ep, n_local * cap, d_model)  35 us
    pallas_call x1, Pallas kernels, rows_pass(): pl.pallas_call(rows_kernel, grid_spec=pltpu.PrefetchScalarGridSpec(num_sc...  29.6 us
  transfers between devices with their start and end apart: 3, of which 2 were waited for; matrix products, arithmetic and copies ran while one was open for 8% of the time, Pallas kernels for 5%

profile of v2, /device:TPU:1, one launch (start us, length us, event | category | flops | bytes accessed | tf_op | source)
XLA Modules:
  0.0 646.3 jit_solution(10783491862378751860)
XLA Ops:
  7.2 0.0 all-reduce.3.cloned.1.call-start
  7.2 1.3 reshape.104.idx_in
  8.5 0.0 copy-start.9
  8.5 0.0 copy-start.8
  8.5 84.7 %gather_rows.1 = (bf16[8,768,768]{2,1,0:T(8,128)(2,1)}, bf16[8,768,768]{2,1,0:T(8,128)(2,1)}, s32[8,1,768]{2,1,0:T(1,128)}) custom-call(bf16[768,768]{1,0:T(8,128)(2,1)} %x_in.1, bf16[768,768]{1,0:T(8,128)(2,1)} %gy_in.1, s32[1,768]{1,0:T(1,128)} %reshape.104.idx_in), custom_call_target="tpu_custom_call" | custom-call | flops 80000000000 | bytes 62914560 | tf_op jit(solution)/shard_map/gather_rows/pallas_call | solution.py:306
  93.2 1.3 copy.21
  94.5 0.0 copy-done.9
  94.5 0.6 broadcast_in_dim.2.own_ref
  95.2 1.9 route.1
  97.1 0.7 slice.6
  97.8 0.0 copy-done.8
  97.8 0.8 copy.15.wg_ref
  98.6 0.1 dynamic_update_slice.3.off_ref
  98.7 0.0 copy-start.2
  98.7 0.0 copy-start.4
  98.7 0.7 copy-done.4
  99.4 19.7 %pick_pass.1 = (bf16[3072,768]{1,0:T(8,128)(2,1)S(1)}, bf16[3072,768]{1,0:T(8,128)(2,1)S(1)}) custom-call(s32[4,16]{1,0:T(4,128)S(1)} %dynamic_update_slice.3.off_ref, s32[8,768]{1,0:T(8,128)S(1)} %copy-done.4, bf16[8,768,768]{2,1,0:T(8,128)(2,1)} %get-tuple-element.23.x_all, bf16[8,768,768]{2,1,0:T(8,128)(2,1)} %get-tuple-element.24.gy_all), custom_call_target="tpu_custom_call" | custom-call | flops 10000000000 | bytes 20971520 | tf_op jit(solution)/shard_map/pick_pass/pallas_call | solution.py:332
  119.2 0.0 copy-done.2
  119.2 0.0 copy-start.5
  119.2 2.2 copy-done.5
  121.4 0.0 copy-start.6
  121.4 2.1 copy-done.6
  123.5 48.7 %grad_pass.1 = (bf16[3072,3072]{1,0:T(8,128)(2,1)}, bf16[3072,3072]{1,0:T(8,128)(2,1)}, f32[2,768,3072]{2,1,0:T(8,128)}, f32[2,3072,768]{2,1,0:T(8,128)}) custom-call(s32[4,16]{1,0:T(4,128)} %copy-done.2, bf16[3072,768]{1,0:T(8,128)(2,1)} %copy-done.5, bf16[3072,768]{1,0:T(8,128)(2,1)} %copy-done.6, bf16[768,16]{1,0:T(8,128)(2,1)} %copy.15.wg_ref, ...), custom_call_target="tpu_custom_call" | custom-call | flops 40000000000 | bytes 62914560 | tf_op jit(solution)/shard_map/grad_pass/pallas_call | solution.py:356
  172.3 0.0 copy-start.3
  172.3 0.0 copy-start.1
  172.3 0.0 all-reduce.3.cloned.1.call-update
  172.3 0.6 copy-done.3
  173.0 0.1 copy.17
  173.0 0.1 add_minimum_fusion
  173.1 0.1 min.18
  173.3 0.0 copy-done.1
  173.3 29.6 %rows_pass.1 = (bf16[3072,768]{1,0:T(8,128)(2,1)S(1)}, bf16[3072,768]{1,0:T(8,128)(2,1)}, f32[768,16]{1,0:T(8,128)S(1)}) custom-call(s32[4,16]{1,0:T(4,128)S(1)} %copy-done.3, bf16[3072,768]{1,0:T(8,128)(2,1)} %copy-done.5, bf16[3072,768]{1,0:T(8,128)(2,1)} %copy-done.6, bf16[3072,3072]{1,0:T(8,128)(2,1)} %get-tuple-element.27.h_ref, ...), custom_call_target="tpu_custom_call" | custom-call | flops 20000000000 | bytes 41943040 | tf_op jit(solution)/shard_map/rows_pass/pallas_call | solution.py:382
  202.9 0.0 copy-start
  202.9 2.2 copy-done
  205.1 17.5 %gather_fusion = bf16[3072,768]{1,0:T(8,128)(2,1)} fusion(bf16[3072,768]{1,0:T(8,128)(2,1)} %copy-done, s32[3072]{0:T(1024)S(1)} %broadcast_clamp_fusion), kind=kCustom, calls=%fused_computation | custom fusion | bytes 9449472 | tf_op jit(solution)/shard_map/gather | solution.py:424
  222.6 4.6 all-to-all-start
  227.1 17.5 %gather_fusion.2 = bf16[3072,768]{1,0:T(8,128)(2,1)} fusion(bf16[3072,768]{1,0:T(8,128)(2,1)} %get-tuple-element.31, s32[3072]{0:T(1024)S(1)} %broadcast_clamp_fusion), kind=kCustom, calls=%fused_computation.2 | custom fusion | bytes 9449472 | tf_op jit(solution)/shard_map/gather | solution.py:424
  244.6 35.1 %all-to-all-done = bf16[8,384,768]{2,1,0:T(8,128)(2,1)} async-done(((bf16[8,384,768]{2,1,0:T(8,128)(2,1)}), bf16[8,384,768]{2,1,0:T(8,128)(2,1)}, u32[]{:S(2)}, u32[]{:S(2)}) %all-to-all-start) | async-done | bytes 4718624 | tf_op jit(solution)/shard_map/all_to_all | solution.py:424
  279.7 0.0 copy-start.10
  279.8 5.7 all-to-all-start.1
  285.5 130.5 %psum.23 = f32[768,16]{1,0:T(8,128)S(1)} all-reduce(f32[768,16]{1,0:T(8,128)S(1)} %get-tuple-element.34), channel_id=1, replica_groups=mesh['dp'=16,'ep'=8] {'dp','ep'}, use_global_device_ids=true, to_apply=%region_2.0 | all-reduce | flops 12288 | bytes 98304 | tf_op jit(solution)/shard_map/psum | solution.py:429
  416.0 0.8 copy.18
  416.8 0.0 copy-done.10
  416.8 6.9 %gather_fusion.1 = bf16[768,768]{1,0:T(8,128)(2,1)} fusion(bf16[3072,768]{1,0:T(8,128)(2,1)} %bitcast.5, s32[1024]{0:T(1024)S(1)} %pad_clamp_fusion), kind=kCustom, calls=%fused_computation.1 | custom fusion | bytes 2362368 | tf_op jit(solution)/shard_map/gather | solution.py:425
  423.7 0.0 all-to-all-done.1
  423.7 6.9 %gather_fusion.3 = bf16[768,768]{1,0:T(8,128)(2,1)} fusion(bf16[3072,768]{1,0:T(8,128)(2,1)} %bitcast.8, s32[1024]{0:T(1024)S(1)} %pad_clamp_fusion), kind=kCustom, calls=%fused_computation.3 | custom fusion | bytes 2362368 | tf_op jit(solution)/shard_map/gather | solution.py:425
  430.6 183.6 %all-reduce.3.cloned.1.call-done = (f32[2,768,3072]{2,1,0:T(8,128)}, f32[2,3072,768]{2,1,0:T(8,128)}) async-done(((f32[2,768,3072]{2,1,0:T(8,128)}, f32[2,3072,768]{2,1,0:T(8,128)}), (f32[2,768,3072]{2,1,0:T(8,128)}, f32[2,3072,768]{2,1,0:T(8,128)})) %all-reduce.3.cloned.1.call-update) | async-done | bytes 37748752 | tf_op jit(solution)/shard_map/psum | solution.py:417
  614.3 0.0 copy-start.7
  614.3 14.0 %copy.25 = f32[2,768,3072]{2,1,0:T(8,128)} copy(f32[2,768,3072]{2,1,0:T(8,128)} %get-tuple-element.49) | data formatting | bytes 37748736
  628.2 4.4 copy-done.7
  632.6 6.8 %copy.26 = f32[2,3072,768]{2,1,0:T(8,128)} copy(f32[2,3072,768]{2,1,0:T(8,128)S(1)} %copy-done.7) | data formatting | bytes 37748736
  (5 shorter events, 0.0 us)
Async XLA Ops:
  7.2 607.1 %all-reduce.3.cloned.1.call-start = ((), (), s32[]{:S(2)}) async-start(), calls=%async_computation.2 | async-start | bytes 75497472 | tf_op jit(solution)/shard_map/psum | solution.py:417
  8.5 86.1 %copy-start.9 = (s32[768]{0:T(1024)S(1)}, s32[768]{0:T(1024)}, u32[]{:S(2)}) copy-start(s32[768]{0:T(1024)} %param.8) | copy-start | bytes 9220
  8.5 89.3 %copy-start.8 = (bf16[768,16]{0,1:T(8,128)(2,1)S(1)}, bf16[768,16]{0,1:T(8,128)(2,1)}, u32[]{:S(2)}) copy-start(bf16[768,16]{0,1:T(8,128)(2,1)} %param.9) | copy-start | bytes 73732
  98.7 20.5 %copy-start.2 = (s32[4,16]{1,0:T(4,128)}, s32[4,16]{1,0:T(4,128)S(1)}, u32[]{:S(2)}) copy-start(s32[4,16]{1,0:T(4,128)S(1)} %dynamic_update_slice.3.off_ref) | copy-start | bytes 772
  98.7 0.7 copy-start.4
  119.2 2.2 copy-start.5
  121.4 2.1 copy-start.6
  172.3 0.7 copy-start.3
  172.3 1.0 copy-start.1
  202.9 2.2 copy-start
  222.6 57.2 %all-to-all-start = ((bf16[8,384,768]{2,1,0:T(8,128)(2,1)}), bf16[8,384,768]{2,1,0:T(8,128)(2,1)}, u32[]{:S(2)}, u32[]{:S(2)}) async-start(bf16[8,384,768]{2,1,0:T(8,128)(2,1)} %bitcast.15), calls=%async_computation | async-start | bytes 9437184 | tf_op jit(solution)/shard_map/all_to_all | solution.py:424
  279.7 137.0 %copy-start.10 = (s32[1,768]{1,0:T(1,128)S(1)}, s32[1,768]{1,0:T(1,128)}, u32[]{:S(2)}) copy-start(s32[1,768]{1,0:T(1,128)} %get-tuple-element.30) | copy-start | bytes 9220
  279.8 144.0 %all-to-all-start.1 = ((bf16[8,384,768]{2,1,0:T(8,128)(2,1)}), bf16[8,384,768]{2,1,0:T(8,128)(2,1)}, u32[]{:S(2)}, u32[]{:S(2)}) async-start(bf16[8,384,768]{2,1,0:T(8,128)(2,1)} %bitcast.14), calls=%async_computation.1 | async-start | bytes 9437184 | tf_op jit(solution)/shard_map/all_to_all | solution.py:424
  614.3 18.4 %copy-start.7 = (f32[2,3072,768]{2,1,0:T(8,128)S(1)}, f32[2,3072,768]{2,1,0:T(8,128)}, u32[]{:S(2)}) copy-start(f32[2,3072,768]{2,1,0:T(8,128)} %get-tuple-element.50) | copy-start | bytes 56623108
Sparse Core Ops, SparseCore 0:
  172.4 441.7 all-reduce.2
